TPU v7x, 512 devices: a whole 4x4x16 slice. The times are simulated.
512 devices in a mesh: row: 32 (over z, y_hi), col: 16 (over y_lo, x, core).
Axes of the slice: x: 4, y: 4 (y_hi: 2, y_lo: 2; y = y_hi * 2 + y_lo), z: 16, core: 2. Of those that a mesh axis runs over, the one named last changes fastest.
Arguments:
- image_embed: float32 [65536, 1152], P(('row', 'col')), may hold values from -150 to 150, as said below
- text_embed: float32 [65536, 1152], P(('row', 'col')), may hold values from -150 to 150
- log_scale: float32 [1], replicated, may hold values from 1.8 to 2.6
- bias: float32 [1], replicated, may hold values from -6 to -3
Outputs:
- loss: float32 [1], replicated
- image_grad: float32 [65536, 1152], P(('row', 'col'))
- text_grad: float32 [65536, 1152], P(('row', 'col'))
Inputs may be any that keep to these rules, and one draw needn't show every extreme that they name: Row i of image_embed and row i of text_embed are correlated.
All inputs are finite; a program needn't handle non-finite values.
Results may differ from a plain program's by a relative error of at most 0.0046.
Values may be sent and summed in bfloat16 or wider, within the bound.
A program may use at most 64 MiB of HBM per device.

v0:
```python
import functools

import jax
import jax.numpy as jnp
from jax import lax
from jax.sharding import Mesh
from jax.sharding import PartitionSpec as P

ROW = ("row_0", "row_1")
COL = ("col_0", "col_1", "col_2")
ROW_COL = ("row_0", "row_1", "col_0", "col_1", "col_2")


def shifted(value, axis, steps):
    count = lax.axis_size(axis)
    pairs = [(source, (source + steps) % count) for source in range(count)]
    return lax.ppermute(value, axis, pairs)


def by_axis(x, axes):
    return functools.reduce(lax.psum, axes, x)


def unit_rows(values):
    inverse = 1.0 / jnp.sqrt(jnp.sum(values * values, axis=1, keepdims=True) + 1e-06)
    return (values * inverse, inverse)


def back_rows(grad_unit, unit, inverse):
    return inverse * (grad_unit - jnp.sum(grad_unit * unit, axis=1, keepdims=True) * unit)


def absorb(img_sum, loss_sum, slab, slab_ids, img_b, img_ids, scale, offset):
    logits = scale * jnp.dot(img_b, slab.T, preferred_element_type=jnp.float32) + offset
    sign = jnp.where(img_ids[:, None] == slab_ids[None, :], 1.0, -1.0).astype(jnp.float32)
    loss_sum = jnp.sum(jax.nn.softplus(-sign * logits))
    weight = (-sign * jax.nn.sigmoid(-sign * logits)).astype(jnp.bfloat16)
    img_sum = jnp.dot(weight, slab, preferred_element_type=jnp.float32)
    term = jnp.dot(weight.T, img_b, preferred_element_type=jnp.float32)
    return (img_sum, loss_sum, term)


def local(image_embed, text_embed, log_scale, bias):
    rows = image_embed.shape[0]
    width = image_embed.shape[1]
    n_row = lax.axis_size(ROW)
    n_col = lax.axis_size(COL)
    at_col = lax.axis_index(COL)
    img_unit, img_inv = unit_rows(image_embed)
    txt_unit, txt_inv = unit_rows(text_embed)
    img_b = img_unit.astype(jnp.bfloat16)
    txt_b = txt_unit.astype(jnp.bfloat16)
    scale = jnp.exp(log_scale[0])
    offset = bias[0]
    img_ids = at_col * rows + jnp.arange(rows, dtype=jnp.int32)
    img_start = jnp.zeros((rows, width), jnp.float32)
    loss_start = jnp.zeros((), jnp.float32)
    piece = lax.all_gather(txt_b, COL, axis=0, tiled=True)
    img_sum = img_start
    loss_sum = loss_start
    slab_ids = jnp.arange(piece.shape[0], dtype=jnp.int32)
    img_sum, loss_sum, term = absorb(
        img_sum, loss_sum, piece, slab_ids, img_b, img_ids, scale, offset
    )
    img_sum, loss_sum, terms = (img_sum, loss_sum, term)

    def pass_owed(step, owed):
        block = (at_col - step - 1) % n_col
        owed = owed + lax.dynamic_slice_in_dim(terms, block * rows, rows, 0)
        return shifted(owed, COL, 1)

    owed = lax.fori_loop(0, n_col - 1, pass_owed, jnp.zeros((rows, width), jnp.float32))
    gathered = owed + lax.dynamic_slice_in_dim(terms, at_col * rows, rows, 0)
    total = by_axis(loss_sum, ROW_COL)
    loss = (total / (rows * n_row * n_col)).reshape(1)
    image_grad = back_rows(scale * img_sum, img_unit, img_inv)
    text_grad = back_rows(scale * gathered, txt_unit, txt_inv)
    return (loss, image_grad, text_grad)


def solution(mesh):
    split = Mesh(
        mesh.devices.reshape(16, 2, 2, 4, 2), ("row_0", "row_1", "col_0", "col_1", "col_2")
    )
    in_specs = (P(ROW_COL, None), P(ROW_COL, None), P(), P())
    out_specs = (P(), P(ROW_COL, None), P(ROW_COL, None))
    return jax.shard_map(local, mesh=split, in_specs=in_specs, out_specs=out_specs, check_vma=False)
```

profile of v0, /device:TPU:24, one launch (start us, length us, event | category | flops | bytes accessed | tf_op | source)
XLA Modules:
  0.0 361.8 jit_solution(10615632890178967644)
XLA Ops:
  7.2 0.0 all-gather.2.cloned.1.call-start
  7.2 1.2 multiply_reduce_fusion.2
  8.4 1.9 multiply_convert_fusion.1
  10.3 0.0 all-gather.2.cloned.1.call-update
  11.7 1.2 multiply_reduce_fusion.3
  12.9 47.2 %all-gather.2.cloned.1.call-done = bf16[2048,1152]{1,0:T(8,128)(2,1)} async-done(((bf16[128,1152]{1,0:T(8,128)(2,1)}), bf16[2048,1152]{1,0:T(8,128)(2,1)}) %all-gather.2.cloned.1.call-update) | async-done | bytes 4718608 | tf_op jit(solution)/shard_map/all_gather | solution.py:58
  60.2 5.2 %fusion.2 = (f32[]{:T(128)}, f32[128,2048]{1,0:T(8,128)S(1)}) fusion(f32[]{:T(128)} %bitcast.5, bf16[2048,1152]{1,0:T(8,128)(2,1)} %all-gather.2.cloned.1.call-done, f32[128,1152]{1,0:T(8,128)} %param.6, f32[128]{0:T(128)S(1)} %add_rsqrt_fusion.1, f32[]{:T(128)} %bitcast, s32[128]{0:T(128)S(1)} %iota_add_fusion), kind=kOutput, calls=%fused_computation.6 | convolution fusion | flops 607682560 | bytes 6358028 | tf_op jit(solution)/shard_map/dot_general | solution.py:34
  65.3 31.9 %psum.35 = f32[]{:T(128)} all-reduce(f32[]{:T(128)} %get-tuple-element.128), channel_id=1, replica_groups=mesh['row_0'=16,'row_1'=2,'col_0'=2,'col_1'=4,'col_2'=2] {'row_0'}, use_global_device_ids=true, to_apply=%region_3.4 | all-reduce | flops 1 | bytes 8 | tf_op jit(solution)/shard_map/psum | solution.py:21
  97.2 7.1 %psum.36 = f32[]{:T(128)} all-reduce(f32[]{:T(128)} %psum.35), channel_id=1, replica_groups=mesh['row_0'=16,'row_1'=2,'col_0'=2,'col_1'=4,'col_2'=2] {'row_1'}, use_global_device_ids=true, to_apply=%region_4.5 | all-reduce | flops 1 | bytes 8 | tf_op jit(solution)/shard_map/psum | solution.py:21
  104.3 5.5 %psum.37 = f32[]{:T(128)} all-reduce(f32[]{:T(128)} %psum.36), channel_id=1, replica_groups=mesh['row_0'=16,'row_1'=2,'col_0'=2,'col_1'=4,'col_2'=2] {'col_0'}, use_global_device_ids=true, to_apply=%region_5.6 | all-reduce | flops 1 | bytes 8 | tf_op jit(solution)/shard_map/psum | solution.py:21
  109.8 10.1 %psum.38 = f32[]{:T(128)} all-reduce(f32[]{:T(128)} %psum.37), channel_id=1, replica_groups=mesh['row_0'=16,'row_1'=2,'col_0'=2,'col_1'=4,'col_2'=2] {'col_1'}, use_global_device_ids=true, to_apply=%region_6.7 | all-reduce | flops 1 | bytes 8 | tf_op jit(solution)/shard_map/psum | solution.py:21
  119.9 3.1 psum.39
  123.0 5.2 %fusion.3 = f32[2048,1152]{1,0:T(8,128)} fusion(f32[128,1152]{1,0:T(8,128)S(1)} %copy-done.1, f32[128]{0:T(128)S(1)} %add_rsqrt_fusion.1, f32[128,2048]{1,0:T(8,128)S(1)} %get-tuple-element.129, s32[128]{0:T(128)S(1)} %iota_add_fusion), kind=kOutput, calls=%fused_computation.22 | convolution fusion | flops 606371840 | bytes 11076608 | tf_op jit(solution)/shard_map/dot_general | solution.py:39
  128.3 0.0 copy-start
  128.3 217.0 %while.15 = (s32[]{:T(128)}, f32[128,1152]{1,0:T(8,128)S(1)}, s32[]{:T(128)}, f32[2048,1152]{1,0:T(8,128)}, s32[]{:T(128)}, /*index=5*/s32[]{:T(128)}, s32[]{:T(...) while((s32[]{:T(128)}, f32[128,1152]{1,0:T(8,128)S(1)}, s32[]{:T(128)}, f32[2048,1152]{1,0:T(8,128)}, ...), condition=%wide.region_10.11_spmd, body=%wide.region_9.10_spmd.sunk | while | flops 147475 | bytes 4129100 | solution.py:72
  128.3 1.2 dynamic-slice_add_fusion.2
  129.5 2.1 collective-permute-start
  131.6 11.2 %collective-permute-done = f32[128,1152]{1,0:T(8,128)S(1)} collective-permute-done((f32[128,1152]{1,0:T(8,128)S(1)}, f32[128,1152]{1,0:T(8,128)S(1)}, u32[]{:S(2)}, u32[]{:S(2)}) %collective-permute-start) | collective-permute-done | bytes 589856 | tf_op jit(solution)/shard_map/while/body/eval_jaxpr/ppermute | solution.py:17
  142.8 1.2 dynamic-slice_add_fusion.2
  144.0 1.9 collective-permute-start
  145.9 11.4 %collective-permute-done = f32[128,1152]{1,0:T(8,128)S(1)} collective-permute-done((f32[128,1152]{1,0:T(8,128)S(1)}, f32[128,1152]{1,0:T(8,128)S(1)}, u32[]{:S(2)}, u32[]{:S(2)}) %collective-permute-start) | collective-permute-done | bytes 589856 | tf_op jit(solution)/shard_map/while/body/eval_jaxpr/ppermute | solution.py:17
  157.3 1.2 dynamic-slice_add_fusion.2
  158.5 1.9 collective-permute-start
  160.4 11.4 %collective-permute-done = f32[128,1152]{1,0:T(8,128)S(1)} collective-permute-done((f32[128,1152]{1,0:T(8,128)S(1)}, f32[128,1152]{1,0:T(8,128)S(1)}, u32[]{:S(2)}, u32[]{:S(2)}) %collective-permute-start) | collective-permute-done | bytes 589856 | tf_op jit(solution)/shard_map/while/body/eval_jaxpr/ppermute | solution.py:17
  171.8 1.2 dynamic-slice_add_fusion.2
  172.9 1.9 collective-permute-start
  174.8 11.4 %collective-permute-done = f32[128,1152]{1,0:T(8,128)S(1)} collective-permute-done((f32[128,1152]{1,0:T(8,128)S(1)}, f32[128,1152]{1,0:T(8,128)S(1)}, u32[]{:S(2)}, u32[]{:S(2)}) %collective-permute-start) | collective-permute-done | bytes 589856 | tf_op jit(solution)/shard_map/while/body/eval_jaxpr/ppermute | solution.py:17
  186.2 1.2 dynamic-slice_add_fusion.2
  187.4 1.9 collective-permute-start
  189.3 11.4 %collective-permute-done = f32[128,1152]{1,0:T(8,128)S(1)} collective-permute-done((f32[128,1152]{1,0:T(8,128)S(1)}, f32[128,1152]{1,0:T(8,128)S(1)}, u32[]{:S(2)}, u32[]{:S(2)}) %collective-permute-start) | collective-permute-done | bytes 589856 | tf_op jit(solution)/shard_map/while/body/eval_jaxpr/ppermute | solution.py:17
  200.7 1.2 dynamic-slice_add_fusion.2
  201.8 1.9 collective-permute-start
  203.8 11.4 %collective-permute-done = f32[128,1152]{1,0:T(8,128)S(1)} collective-permute-done((f32[128,1152]{1,0:T(8,128)S(1)}, f32[128,1152]{1,0:T(8,128)S(1)}, u32[]{:S(2)}, u32[]{:S(2)}) %collective-permute-start) | collective-permute-done | bytes 589856 | tf_op jit(solution)/shard_map/while/body/eval_jaxpr/ppermute | solution.py:17
  215.2 1.2 dynamic-slice_add_fusion.2
  216.3 1.9 collective-permute-start
  218.2 11.4 %collective-permute-done = f32[128,1152]{1,0:T(8,128)S(1)} collective-permute-done((f32[128,1152]{1,0:T(8,128)S(1)}, f32[128,1152]{1,0:T(8,128)S(1)}, u32[]{:S(2)}, u32[]{:S(2)}) %collective-permute-start) | collective-permute-done | bytes 589856 | tf_op jit(solution)/shard_map/while/body/eval_jaxpr/ppermute | solution.py:17
  229.6 1.2 dynamic-slice_add_fusion.2
  230.8 1.9 collective-permute-start
  232.7 11.4 %collective-permute-done = f32[128,1152]{1,0:T(8,128)S(1)} collective-permute-done((f32[128,1152]{1,0:T(8,128)S(1)}, f32[128,1152]{1,0:T(8,128)S(1)}, u32[]{:S(2)}, u32[]{:S(2)}) %collective-permute-start) | collective-permute-done | bytes 589856 | tf_op jit(solution)/shard_map/while/body/eval_jaxpr/ppermute | solution.py:17
  244.1 1.2 dynamic-slice_add_fusion.2
  245.2 1.9 collective-permute-start
  247.2 11.4 %collective-permute-done = f32[128,1152]{1,0:T(8,128)S(1)} collective-permute-done((f32[128,1152]{1,0:T(8,128)S(1)}, f32[128,1152]{1,0:T(8,128)S(1)}, u32[]{:S(2)}, u32[]{:S(2)}) %collective-permute-start) | collective-permute-done | bytes 589856 | tf_op jit(solution)/shard_map/while/body/eval_jaxpr/ppermute | solution.py:17
  258.5 1.2 dynamic-slice_add_fusion.2
  259.7 1.9 collective-permute-start
  261.6 11.4 %collective-permute-done = f32[128,1152]{1,0:T(8,128)S(1)} collective-permute-done((f32[128,1152]{1,0:T(8,128)S(1)}, f32[128,1152]{1,0:T(8,128)S(1)}, u32[]{:S(2)}, u32[]{:S(2)}) %collective-permute-start) | collective-permute-done | bytes 589856 | tf_op jit(solution)/shard_map/while/body/eval_jaxpr/ppermute | solution.py:17
  273.0 1.2 dynamic-slice_add_fusion.2
  274.2 1.9 collective-permute-start
  276.1 11.4 %collective-permute-done = f32[128,1152]{1,0:T(8,128)S(1)} collective-permute-done((f32[128,1152]{1,0:T(8,128)S(1)}, f32[128,1152]{1,0:T(8,128)S(1)}, u32[]{:S(2)}, u32[]{:S(2)}) %collective-permute-start) | collective-permute-done | bytes 589856 | tf_op jit(solution)/shard_map/while/body/eval_jaxpr/ppermute | solution.py:17
  287.5 1.2 dynamic-slice_add_fusion.2
  288.6 1.9 collective-permute-start
  290.5 11.4 %collective-permute-done = f32[128,1152]{1,0:T(8,128)S(1)} collective-permute-done((f32[128,1152]{1,0:T(8,128)S(1)}, f32[128,1152]{1,0:T(8,128)S(1)}, u32[]{:S(2)}, u32[]{:S(2)}) %collective-permute-start) | collective-permute-done | bytes 589856 | tf_op jit(solution)/shard_map/while/body/eval_jaxpr/ppermute | solution.py:17
  301.9 1.2 dynamic-slice_add_fusion.2
  303.1 1.9 collective-permute-start
  305.0 11.4 %collective-permute-done = f32[128,1152]{1,0:T(8,128)S(1)} collective-permute-done((f32[128,1152]{1,0:T(8,128)S(1)}, f32[128,1152]{1,0:T(8,128)S(1)}, u32[]{:S(2)}, u32[]{:S(2)}) %collective-permute-start) | collective-permute-done | bytes 589856 | tf_op jit(solution)/shard_map/while/body/eval_jaxpr/ppermute | solution.py:17
  316.4 1.2 dynamic-slice_add_fusion.2
  317.5 1.9 collective-permute-start
  319.5 11.4 %collective-permute-done = f32[128,1152]{1,0:T(8,128)S(1)} collective-permute-done((f32[128,1152]{1,0:T(8,128)S(1)}, f32[128,1152]{1,0:T(8,128)S(1)}, u32[]{:S(2)}, u32[]{:S(2)}) %collective-permute-start) | collective-permute-done | bytes 589856 | tf_op jit(solution)/shard_map/while/body/eval_jaxpr/ppermute | solution.py:17
  330.9 1.2 dynamic-slice_add_fusion.2
  332.0 1.9 collective-permute-start
  333.9 11.4 %collective-permute-done = f32[128,1152]{1,0:T(8,128)S(1)} collective-permute-done((f32[128,1152]{1,0:T(8,128)S(1)}, f32[128,1152]{1,0:T(8,128)S(1)}, u32[]{:S(2)}, u32[]{:S(2)}) %collective-permute-start) | collective-permute-done | bytes 589856 | tf_op jit(solution)/shard_map/while/body/eval_jaxpr/ppermute | solution.py:17
  345.3 1.3 multiply_reduce_fusion
  346.6 2.1 subtract_multiply_fusion
  349.4 3.5 multiply_reduce_fusion.1
  352.8 1.0 subtract_multiply_fusion.1
  (7 shorter events, 0.1 us)
Async XLA Ops:
  7.2 53.0 %all-gather.2.cloned.1.call-start = ((), (), s32[]{:S(2)}) async-start(), calls=%async_computation | async-start | bytes 5013504 | tf_op jit(solution)/shard_map/all_gather | solution.py:58
  10.3 112.7 %copy-start.1 = (f32[128,1152]{1,0:T(8,128)S(1)}, f32[128,1152]{1,0:T(8,128)}, u32[]{:S(2)}) copy-start(f32[128,1152]{1,0:T(8,128)} %param.6) | copy-start | bytes 1769476
  128.3 217.0 %copy-start = (f32[128,1152]{1,0:T(8,128)S(1)}, f32[128,1152]{1,0:T(8,128)}, u32[]{:S(2)}) copy-start(f32[128,1152]{1,0:T(8,128)} %param.7) | copy-start | bytes 1769476
  129.5 13.3 %collective-permute-start = (f32[128,1152]{1,0:T(8,128)S(1)}, f32[128,1152]{1,0:T(8,128)S(1)}, u32[]{:S(2)}, u32[]{:S(2)}) collective-permute-start(f32[128,1152]{1,0:T(8,128)S(1)} %dynamic-slice_add_fusion.2), channel_id=1, source_target_pairs={{0,1},{1,2},{2,3},{3,4},{4,5},{5,6},{6,7},{7,8},{8,9},{9,10},{10,1... | collective-permute-start | bytes 1769480 | tf_op jit(solution)/shard_map/while/body/eval_jaxpr/ppermute | solution.py:17
  144.0 13.3 %collective-permute-start = (f32[128,1152]{1,0:T(8,128)S(1)}, f32[128,1152]{1,0:T(8,128)S(1)}, u32[]{:S(2)}, u32[]{:S(2)}) collective-permute-start(f32[128,1152]{1,0:T(8,128)S(1)} %dynamic-slice_add_fusion.2), channel_id=1, source_target_pairs={{0,1},{1,2},{2,3},{3,4},{4,5},{5,6},{6,7},{7,8},{8,9},{9,10},{10,1... | collective-permute-start | bytes 1769480 | tf_op jit(solution)/shard_map/while/body/eval_jaxpr/ppermute | solution.py:17
  158.5 13.3 %collective-permute-start = (f32[128,1152]{1,0:T(8,128)S(1)}, f32[128,1152]{1,0:T(8,128)S(1)}, u32[]{:S(2)}, u32[]{:S(2)}) collective-permute-start(f32[128,1152]{1,0:T(8,128)S(1)} %dynamic-slice_add_fusion.2), channel_id=1, source_target_pairs={{0,1},{1,2},{2,3},{3,4},{4,5},{5,6},{6,7},{7,8},{8,9},{9,10},{10,1... | collective-permute-start | bytes 1769480 | tf_op jit(solution)/shard_map/while/body/eval_jaxpr/ppermute | solution.py:17
  172.9 13.3 %collective-permute-start = (f32[128,1152]{1,0:T(8,128)S(1)}, f32[128,1152]{1,0:T(8,128)S(1)}, u32[]{:S(2)}, u32[]{:S(2)}) collective-permute-start(f32[128,1152]{1,0:T(8,128)S(1)} %dynamic-slice_add_fusion.2), channel_id=1, source_target_pairs={{0,1},{1,2},{2,3},{3,4},{4,5},{5,6},{6,7},{7,8},{8,9},{9,10},{10,1... | collective-permute-start | bytes 1769480 | tf_op jit(solution)/shard_map/while/body/eval_jaxpr/ppermute | solution.py:17
  187.4 13.3 %collective-permute-start = (f32[128,1152]{1,0:T(8,128)S(1)}, f32[128,1152]{1,0:T(8,128)S(1)}, u32[]{:S(2)}, u32[]{:S(2)}) collective-permute-start(f32[128,1152]{1,0:T(8,128)S(1)} %dynamic-slice_add_fusion.2), channel_id=1, source_target_pairs={{0,1},{1,2},{2,3},{3,4},{4,5},{5,6},{6,7},{7,8},{8,9},{9,10},{10,1... | collective-permute-start | bytes 1769480 | tf_op jit(solution)/shard_map/while/body/eval_jaxpr/ppermute | solution.py:17
  201.8 13.3 %collective-permute-start = (f32[128,1152]{1,0:T(8,128)S(1)}, f32[128,1152]{1,0:T(8,128)S(1)}, u32[]{:S(2)}, u32[]{:S(2)}) collective-permute-start(f32[128,1152]{1,0:T(8,128)S(1)} %dynamic-slice_add_fusion.2), channel_id=1, source_target_pairs={{0,1},{1,2},{2,3},{3,4},{4,5},{5,6},{6,7},{7,8},{8,9},{9,10},{10,1... | collective-permute-start | bytes 1769480 | tf_op jit(solution)/shard_map/while/body/eval_jaxpr/ppermute | solution.py:17
  216.3 13.3 %collective-permute-start = (f32[128,1152]{1,0:T(8,128)S(1)}, f32[128,1152]{1,0:T(8,128)S(1)}, u32[]{:S(2)}, u32[]{:S(2)}) collective-permute-start(f32[128,1152]{1,0:T(8,128)S(1)} %dynamic-slice_add_fusion.2), channel_id=1, source_target_pairs={{0,1},{1,2},{2,3},{3,4},{4,5},{5,6},{6,7},{7,8},{8,9},{9,10},{10,1... | collective-permute-start | bytes 1769480 | tf_op jit(solution)/shard_map/while/body/eval_jaxpr/ppermute | solution.py:17
  230.8 13.3 %collective-permute-start = (f32[128,1152]{1,0:T(8,128)S(1)}, f32[128,1152]{1,0:T(8,128)S(1)}, u32[]{:S(2)}, u32[]{:S(2)}) collective-permute-start(f32[128,1152]{1,0:T(8,128)S(1)} %dynamic-slice_add_fusion.2), channel_id=1, source_target_pairs={{0,1},{1,2},{2,3},{3,4},{4,5},{5,6},{6,7},{7,8},{8,9},{9,10},{10,1... | collective-permute-start | bytes 1769480 | tf_op jit(solution)/shard_map/while/body/eval_jaxpr/ppermute | solution.py:17
  245.2 13.3 %collective-permute-start = (f32[128,1152]{1,0:T(8,128)S(1)}, f32[128,1152]{1,0:T(8,128)S(1)}, u32[]{:S(2)}, u32[]{:S(2)}) collective-permute-start(f32[128,1152]{1,0:T(8,128)S(1)} %dynamic-slice_add_fusion.2), channel_id=1, source_target_pairs={{0,1},{1,2},{2,3},{3,4},{4,5},{5,6},{6,7},{7,8},{8,9},{9,10},{10,1... | collective-permute-start | bytes 1769480 | tf_op jit(solution)/shard_map/while/body/eval_jaxpr/ppermute | solution.py:17
  259.7 13.3 %collective-permute-start = (f32[128,1152]{1,0:T(8,128)S(1)}, f32[128,1152]{1,0:T(8,128)S(1)}, u32[]{:S(2)}, u32[]{:S(2)}) collective-permute-start(f32[128,1152]{1,0:T(8,128)S(1)} %dynamic-slice_add_fusion.2), channel_id=1, source_target_pairs={{0,1},{1,2},{2,3},{3,4},{4,5},{5,6},{6,7},{7,8},{8,9},{9,10},{10,1... | collective-permute-start | bytes 1769480 | tf_op jit(solution)/shard_map/while/body/eval_jaxpr/ppermute | solution.py:17
  274.2 13.3 %collective-permute-start = (f32[128,1152]{1,0:T(8,128)S(1)}, f32[128,1152]{1,0:T(8,128)S(1)}, u32[]{:S(2)}, u32[]{:S(2)}) collective-permute-start(f32[128,1152]{1,0:T(8,128)S(1)} %dynamic-slice_add_fusion.2), channel_id=1, source_target_pairs={{0,1},{1,2},{2,3},{3,4},{4,5},{5,6},{6,7},{7,8},{8,9},{9,10},{10,1... | collective-permute-start | bytes 1769480 | tf_op jit(solution)/shard_map/while/body/eval_jaxpr/ppermute | solution.py:17
  288.6 13.3 %collective-permute-start = (f32[128,1152]{1,0:T(8,128)S(1)}, f32[128,1152]{1,0:T(8,128)S(1)}, u32[]{:S(2)}, u32[]{:S(2)}) collective-permute-start(f32[128,1152]{1,0:T(8,128)S(1)} %dynamic-slice_add_fusion.2), channel_id=1, source_target_pairs={{0,1},{1,2},{2,3},{3,4},{4,5},{5,6},{6,7},{7,8},{8,9},{9,10},{10,1... | collective-permute-start | bytes 1769480 | tf_op jit(solution)/shard_map/while/body/eval_jaxpr/ppermute | solution.py:17
  303.1 13.3 %collective-permute-start = (f32[128,1152]{1,0:T(8,128)S(1)}, f32[128,1152]{1,0:T(8,128)S(1)}, u32[]{:S(2)}, u32[]{:S(2)}) collective-permute-start(f32[128,1152]{1,0:T(8,128)S(1)} %dynamic-slice_add_fusion.2), channel_id=1, source_target_pairs={{0,1},{1,2},{2,3},{3,4},{4,5},{5,6},{6,7},{7,8},{8,9},{9,10},{10,1... | collective-permute-start | bytes 1769480 | tf_op jit(solution)/shard_map/while/body/eval_jaxpr/ppermute | solution.py:17
  317.5 13.3 %collective-permute-start = (f32[128,1152]{1,0:T(8,128)S(1)}, f32[128,1152]{1,0:T(8,128)S(1)}, u32[]{:S(2)}, u32[]{:S(2)}) collective-permute-start(f32[128,1152]{1,0:T(8,128)S(1)} %dynamic-slice_add_fusion.2), channel_id=1, source_target_pairs={{0,1},{1,2},{2,3},{3,4},{4,5},{5,6},{6,7},{7,8},{8,9},{9,10},{10,1... | collective-permute-start | bytes 1769480 | tf_op jit(solution)/shard_map/while/body/eval_jaxpr/ppermute | solution.py:17
  332.0 13.3 %collective-permute-start = (f32[128,1152]{1,0:T(8,128)S(1)}, f32[128,1152]{1,0:T(8,128)S(1)}, u32[]{:S(2)}, u32[]{:S(2)}) collective-permute-start(f32[128,1152]{1,0:T(8,128)S(1)} %dynamic-slice_add_fusion.2), channel_id=1, source_target_pairs={{0,1},{1,2},{2,3},{3,4},{4,5},{5,6},{6,7},{7,8},{8,9},{9,10},{10,1... | collective-permute-start | bytes 1769480 | tf_op jit(solution)/shard_map/while/body/eval_jaxpr/ppermute | solution.py:17
Sparse Core Ops, SparseCore 0:
  10.7 49.4 all-gather.1
where the time goes:
time: 363 us; the launch traced here: 362 us
  waiting for transfers between devices  218 us (60%)
  blocking collectives  57.7 us (16%)
  starting transfers between devices  29 us (8%)
  other arithmetic  26 us (7%)
  between operations  17.3 us (5%)
  matrix products  13.9 us (4%)
    ppermute x15, waiting for transfers between devices, shifted(): return lax.ppermute(value, axis, pairs)  171 us
    psum x5, blocking collectives, by_axis(): return functools.reduce(lax.psum, axes, x)  57.7 us
    all_gather x1, waiting for transfers between devices, local(): piece = lax.all_gather(txt_b, COL, axis=0, tiled=True)  47.2 us
    ppermute x15, starting transfers between devices, shifted(): return lax.ppermute(value, axis, pairs)  29 us
    add x15, other arithmetic, pass_owed(): owed = owed + lax.dynamic_slice_in_dim(terms, block * rows, rows, 0)  17.3 us
  transfers between devices with their start and end apart: 16, of which 16 were waited for; matrix products, arithmetic and copies ran while one was open for 0% of the time, Pallas kernels for 0%

commit v1 on v0

v1 whole, which is shorter than its diff:
```python
import functools

import jax
import jax.numpy as jnp
from jax import lax
from jax.experimental import pallas as pl
from jax.experimental.pallas import tpu as pltpu
from jax.sharding import Mesh
from jax.sharding import PartitionSpec as P

AXES = ("z", "yh", "yl", "x", "c")
MESH = pl.DeviceIdType.MESH
BF = jnp.bfloat16
F32 = jnp.float32
CHUNK = 384


def nt_dot(a, b):
    return lax.dot_general(a, b, (((1,), (1,)), ((), ())), preferred_element_type=F32)


def tn_dot(a, b):
    return lax.dot_general(a, b, (((0,), (0,)), ((), ())), preferred_element_type=F32)


def kernel(
    log_scale_ref, bias_ref, img_hbm, txt_hbm,
    loss_ref, img_grad, txt_grad,
    img_x, txt_x, img_inv, txt_inv, img_all, txt_all, logit, weight,
    own_p, hold_p, own_q, hold_q,
    out_right, out_left, out_opp, out_sib, out_diag, out_comb, out_part,
    way_x, fin_left, fin_right, way_t, fin_sib, fin_part,
    loss_box, loss_out, loss_in1, loss_in2, loss_in3,
    load_sem, send_sem, recv_sem, lsend_sem, lrecv_sem, near_sem,
):
    rows, width = img_x.shape
    half = rows // 2
    nz, nyh, nx = lax.axis_size("z"), lax.axis_size("yh"), lax.axis_size("x")
    ny = 2 * nyh
    z, yh, yl = lax.axis_index("z"), lax.axis_index("yh"), lax.axis_index("yl")
    x, c = lax.axis_index("x"), lax.axis_index("c")
    y = yh * 2 + yl

    def at_x(step, core=0):
        return {"x": lax.rem(x + step, nx), "c": lax.rem(c + core, 2)}

    def at_y(step):
        there = lax.rem(y + step, ny)
        return {"yh": there // 2, "yl": lax.rem(there, 2)}

    def at_z(step):
        return {"z": lax.rem(z + step, nz)}

    right, left, sibling = at_x(1), at_x(nx - 1), at_x(0, 1)
    partner = {"yl": 1 - yl}

    load_img = pltpu.make_async_copy(img_hbm, img_x, load_sem.at[0])
    load_txt = pltpu.make_async_copy(txt_hbm, txt_x, load_sem.at[1])
    load_img.start()
    load_txt.start()

    around = [right, left, sibling, at_y(1), at_y(ny - 1), at_z(1), at_z(nz - 1)]
    barrier = pltpu.get_barrier_semaphore()
    for peer in around:
        pl.semaphore_signal(barrier, inc=1, device_id=peer, device_id_type=MESH)

    def send(index, source, target, peer):
        copy = pltpu.make_async_remote_copy(
            src_ref=source, dst_ref=target, send_sem=send_sem.at[index], recv_sem=recv_sem.at[index],
            device_id=peer, device_id_type=MESH,
        )
        copy.start()
        return copy

    def normalize(values, inverse, packed):
        step = 32
        for start in range(0, rows, step):
            part = values[start : start + step, :]
            inv = lax.rsqrt(jnp.sum(part * part, axis=1, keepdims=True) + 1e-06)
            inverse[start : start + step, :] = inv
            packed[start : start + step, :] = (part * inv).astype(BF)

    a, b = pl.ds(0, half), pl.ds(half, half)

    def slot(index, offset=0, size=None):
        return pl.ds(index * rows + offset, rows if size is None else size)

    load_img.wait()
    normalize(img_x, img_inv, img_all)
    pl.semaphore_wait(barrier, len(around))
    right_a = send(0, img_all.at[a], img_all.at[slot(1, 0, half)], right)
    left_b = send(2, img_all.at[b], img_all.at[slot(2, half, half)], left)
    right_b = send(1, img_all.at[b], img_all.at[slot(1, half, half)], right)
    left_a = send(3, img_all.at[a], img_all.at[slot(2, 0, half)], left)
    load_txt.wait()
    normalize(txt_x, txt_inv, txt_all)
    txt_part = send(7, txt_all.at[slot(0)], txt_all.at[slot(2)], partner)
    txt_sib = send(6, txt_all.at[slot(0)], txt_all.at[slot(1)], sibling)

    for index, group in enumerate((around, [at_z(2), at_z(nz - 2), sibling], [at_z(4), at_z(nz - 4)])):
        for peer in group:
            pl.semaphore_signal(near_sem.at[index], inc=1, device_id=peer, device_id_type=MESH)
        pl.semaphore_wait(near_sem.at[index], len(group))

    right_a.wait_recv()
    pass_right = send(4, img_all.at[slot(1, 0, half)], img_all.at[slot(3, 0, half)], right)
    left_b.wait_recv()
    pass_left = send(5, img_all.at[slot(2, half, half)], img_all.at[slot(3, half, half)], left)
    txt_part.wait_recv()
    txt_diag = send(8, txt_all.at[slot(2)], txt_all.at[slot(3)], sibling)

    log_scale = jnp.full((1, 4 * rows), log_scale_ref[0], F32)
    scale = jnp.exp(log_scale)
    offset = jnp.full((1, 4 * rows), bias_ref[0], F32)

    def weights(index):
        logits = scale * nt_dot(img_all[slot(index), :], txt_all[...]) + offset
        logit[slot(index), :] = logits
        small = jnp.exp(-jnp.abs(logits))
        inv = 1.0 / (1.0 + small)
        value = jnp.where(logits >= 0, 1.0, small) * inv
        if index == 0:
            mine = (lax.broadcasted_iota(jnp.int32, value.shape, 0)
                    == lax.broadcasted_iota(jnp.int32, value.shape, 1))
            value = jnp.where(mine, -jnp.where(logits >= 0, small, 1.0) * inv, value)
        weight[slot(index), :] = value.astype(BF)

    def img_term(index, start):
        return jnp.dot(weight[slot(index), :], txt_all[:, start : start + CHUNK], preferred_element_type=F32)

    def txt_term(index, start):
        block = weight[:, index * rows : (index + 1) * rows]
        return tn_dot(block, img_all[:, start : start + CHUNK])

    chunks = [(start, slice(start, start + CHUNK)) for start in range(0, width, CHUNK)]

    txt_sib.wait_recv()
    txt_diag.wait_recv()
    weights(0)
    right_b.wait_recv()
    left_a.wait_recv()
    weights(1)
    weights(2)
    for start, cols in chunks:
        term = img_term(2, start)
        hold_p[0:half, cols] = term[0:half]
        out_right[:, cols] = term[half:].astype(BF)
    to_right = send(11, out_right, fin_left.at[b], right)
    for start, cols in chunks:
        term = img_term(1, start)
        hold_p[half:, cols] = term[half:]
        out_left[:, cols] = term[0:half].astype(BF)
    to_left = send(12, out_left, fin_right.at[a], left)
    for start, cols in chunks:
        own_p[:, cols] = img_term(0, start)

    pass_right.wait_recv()
    pass_left.wait_recv()
    weights(3)
    for start, cols in chunks:
        out_opp[:, cols] = img_term(3, start).astype(BF)
    opp_right = send(9, out_opp.at[a], way_x.at[a], right)
    opp_left = send(10, out_opp.at[b], way_x.at[b], left)
    for start, cols in chunks:
        out_diag[:, cols] = txt_term(3, start).astype(BF)
    diag = send(15, out_diag, way_t, sibling)
    for start, cols in chunks:
        out_sib[:, cols] = txt_term(1, start).astype(BF)
    sib = send(16, out_sib, fin_sib, sibling)
    for start, cols in chunks:
        hold_q[:, cols] = txt_term(2, start)
    for start, cols in chunks:
        own_q[:, cols] = txt_term(0, start)

    total = jnp.zeros((8, 4 * rows), F32)
    step = 64
    for start in range(0, 4 * rows, step):
        logits = logit[start : start + step, :]
        flip = jnp.maximum(logits, 0.0)
        if start < rows:
            mine = (lax.broadcasted_iota(jnp.int32, logits.shape, 0) + start
                    == lax.broadcasted_iota(jnp.int32, logits.shape, 1))
            flip = jnp.where(mine, jnp.maximum(-logits, 0.0), flip)
        terms = flip + jnp.log1p(jnp.exp(-jnp.abs(logits)))
        total = total + jnp.sum(terms.reshape(step // 8, 8, 4 * rows), axis=0)
    total = jnp.sum(total, axis=0, keepdims=True)
    total = sum(total[:, k * rows : (k + 1) * rows] for k in range(4))

    lsent = []

    def spread(base, value, stage, inbox, peers):
        loss_out[stage] = value
        copies = []
        for k, peer in enumerate(peers):
            copy = pltpu.make_async_remote_copy(
                src_ref=loss_out.at[stage], dst_ref=inbox.at[k], send_sem=lsend_sem.at[base + k],
                recv_sem=lrecv_sem.at[base + k], device_id=peer, device_id_type=MESH,
            )
            copy.start()
            copies.append(copy)
        lsent.extend(copies)
        return copies

    def gather(value, copies, inbox):
        for k, copy in enumerate(copies):
            copy.wait_recv()
            value = value + inbox[k]
        return value

    plane = [at_x(step, core) for core in range(2) for step in range(nx) if step or core]
    first = spread(0, total, 0, loss_in1, plane)

    diag.wait_recv()
    for start, cols in chunks:
        out_part[:, cols] = (hold_q[:, cols] + way_t[:, cols].astype(F32)).astype(BF)
    part = send(17, out_part, fin_part, partner)

    total = gather(total, first, loss_in1)
    second = spread(len(plane), total, 1, loss_in2, [at_y(step) for step in range(1, ny)])

    opp_right.wait_recv()
    out_comb[a] = (hold_p[a] + way_x[a].astype(F32)).astype(BF)
    comb_right = send(13, out_comb.at[a], fin_left.at[a], right)
    opp_left.wait_recv()
    out_comb[b] = (hold_p[b] + way_x[b].astype(F32)).astype(BF)
    comb_left = send(14, out_comb.at[b], fin_right.at[b], left)

    total = gather(total, second, loss_in2)
    third = spread(len(plane) + ny - 1, total, 2, loss_in3, [at_z(step) for step in range(1, nz)])

    scale = jnp.exp(jnp.full((1, width), log_scale_ref[0], F32))

    def back(own, one, two, values, inverse, target):
        step = 32
        for start in range(0, rows, step):
            r = slice(start, start + step)
            grad = scale * (own[r, :] + one[r, :].astype(F32) + two[r, :].astype(F32))
            inv = inverse[r, :]
            unit = values[r, :] * inv
            target[r, :] = inv * (grad - jnp.sum(grad * unit, axis=1, keepdims=True) * unit)

    to_right.wait_recv()
    to_left.wait_recv()
    sib.wait_recv()
    part.wait_recv()
    back(own_q, fin_sib, fin_part, txt_x, txt_inv, txt_grad)
    comb_right.wait_recv()
    comb_left.wait_recv()
    back(own_p, fin_left, fin_right, img_x, img_inv, img_grad)

    total = gather(total, third, loss_in3)
    count = rows * 4 * nx * nyh * nz
    loss_ref[0] = jnp.sum(total) * (1.0 / count)

    for copy in (
        right_a, left_b, right_b, left_a, txt_part, txt_sib, pass_right, pass_left, txt_diag, to_right, to_left,
        opp_right, opp_left, diag, sib, part, comb_right, comb_left, *lsent,
    ):
        copy.wait_send()


def local(image_embed, text_embed, log_scale, bias):
    rows, width = image_embed.shape
    half = rows // 2
    nx, ny, nz = lax.axis_size("x"), 2 * lax.axis_size("yh"), lax.axis_size("z")
    peers = 2 * nx - 1 + ny - 1 + nz - 1
    smem = pl.BlockSpec(memory_space=pltpu.SMEM)
    hbm = pl.BlockSpec(memory_space=pltpu.HBM)
    vmem = pl.BlockSpec(memory_space=pltpu.VMEM)
    block = pltpu.VMEM((rows, width), BF)
    wide = pltpu.VMEM((rows, width), F32)
    part = pltpu.VMEM((half, width), BF)
    column = pltpu.VMEM((rows, 1), F32)
    return pl.pallas_call(
        kernel,
        out_shape=(
            jax.ShapeDtypeStruct((1,), F32),
            jax.ShapeDtypeStruct((rows, width), F32),
            jax.ShapeDtypeStruct((rows, width), F32),
        ),
        in_specs=[smem, smem, hbm, hbm],
        out_specs=(smem, vmem, vmem),
        scratch_shapes=[
            wide, wide, column, column,
            pltpu.VMEM((4 * rows, width), BF), pltpu.VMEM((4 * rows, width), BF),
            pltpu.VMEM((4 * rows, 4 * rows), F32), pltpu.VMEM((4 * rows, 4 * rows), BF),
            wide, wide, wide, wide,
            part, part, block, block, block, block, block,
            block, block, block, block, block, block,
            pltpu.VMEM((1, 128), F32), pltpu.VMEM((3, 1, 128), F32),
            pltpu.VMEM((2 * nx - 1, 1, 128), F32), pltpu.VMEM((ny - 1, 1, 128), F32),
            pltpu.VMEM((max(nz - 1, 1), 1, 128), F32),
            pltpu.SemaphoreType.DMA((2,)), pltpu.SemaphoreType.DMA((18,)), pltpu.SemaphoreType.DMA((18,)),
            pltpu.SemaphoreType.DMA((peers,)), pltpu.SemaphoreType.DMA((peers,)),
            pltpu.SemaphoreType.REGULAR((3,)),
        ],
        compiler_params=pltpu.CompilerParams(
            collective_id=0, has_side_effects=True, vmem_limit_bytes=48 * 1024 * 1024
        ),
        name="siglip",
    )(log_scale, bias, image_embed, text_embed)


def solution(mesh):
    split = Mesh(mesh.devices.reshape(16, 2, 2, 4, 2), AXES)
    rows = P(AXES, None)
    return jax.shard_map(
        local, mesh=split, in_specs=(rows, rows, P(), P()), out_specs=(P(), rows, rows), check_vma=False
    )
```

time: 363 us -> 53.1 us (0.15)
  the two profiles are of different devices: /device:TPU:24 before, /device:TPU:1 now
where the time goes in v1:
time: 53.1 us; the launch traced here: 52.8 us
  Pallas kernels  45.4 us (85%)
  local copies, waits for them, and re-layouts  3.75 us (7%)
  between operations  3.7 us (7%)
    pallas_call x1, Pallas kernels, local(): pl.pallas_call(kernel, out_shape=(jax.ShapeDtypeStruct((1,), F32), jax.Sh...  45.4 us
    unnamed x6, local copies, waits for them, and re-layouts  3.75 us

profile of v1, /device:TPU:1, one launch (start us, length us, event | category | flops | bytes accessed | tf_op | source)
XLA Modules:
  0.0 52.8 jit_solution(3522599497988267876)
XLA Ops:
  1.9 0.0 copy-start
  1.9 1.1 %copy-done = f32[128,1152]{1,0:T(8,128)S(1)} copy-done((f32[128,1152]{1,0:T(8,128)S(1)}, f32[128,1152]{1,0:T(8,128)}, u32[]{:S(2)}) %copy-start) | copy-done | bytes 589848
  3.0 0.0 copy-start.1
  3.0 1.1 %copy-done.1 = f32[128,1152]{1,0:T(8,128)S(1)} copy-done((f32[128,1152]{1,0:T(8,128)S(1)}, f32[128,1152]{1,0:T(8,128)}, u32[]{:S(2)}) %copy-start.1) | copy-done | bytes 589848
  4.1 45.4 %siglip.1 = (f32[1]{0:T(128)}, f32[128,1152]{1,0:T(8,128)S(1)}, f32[128,1152]{1,0:T(8,128)S(1)}) custom-call(f32[1]{0:T(128)S(6)} %copy.10.log_scale_ref, f32[1]{0:T(128)S(6)} %copy.11.bias_ref, f32[128,1152]{1,0:T(8,128)S(1)} %copy-done, f32[128,1152]{1,0:T(8,128)S(1)} %copy-done.1), custom_call_target="tpu_custom_call" | custom-call | tf_op jit(solution)/shard_map/siglip/pallas_call | solution.py:274
  50.1 0.8 %copy.13 = f32[128,1152]{1,0:T(8,128)} copy(f32[128,1152]{1,0:T(8,128)S(1)} %get-tuple-element.7) | data formatting | bytes 1179648
  50.9 0.8 %copy.14 = f32[128,1152]{1,0:T(8,128)} copy(f32[128,1152]{1,0:T(8,128)S(1)} %get-tuple-element.8) | data formatting | bytes 1179648
Async XLA Ops:
  1.9 1.1 %copy-start = (f32[128,1152]{1,0:T(8,128)S(1)}, f32[128,1152]{1,0:T(8,128)}, u32[]{:S(2)}) copy-start(f32[128,1152]{1,0:T(8,128)} %img_hbm.1) | copy-start | bytes 1769476
  3.0 1.1 %copy-start.1 = (f32[128,1152]{1,0:T(8,128)S(1)}, f32[128,1152]{1,0:T(8,128)}, u32[]{:S(2)}) copy-start(f32[128,1152]{1,0:T(8,128)} %txt_hbm.1) | copy-start | bytes 1769476

commit v2 on v1

--- a/solution.py
+++ b/solution.py
@@ -15,6 +15,10 @@
 CHUNK = 384
 
 
+def in_hbm(value):
+    return pltpu.with_memory_space_constraint(value, pltpu.HBM)
+
+
 def nt_dot(a, b):
     return lax.dot_general(a, b, (((1,), (1,)), ((), ())), preferred_element_type=F32)
 
@@ -30,7 +34,7 @@
     own_p, hold_p, own_q, hold_q,
     out_right, out_left, out_opp, out_sib, out_diag, out_comb, out_part,
     way_x, fin_left, fin_right, way_t, fin_sib, fin_part,
-    loss_box, loss_out, loss_in1, loss_in2, loss_in3,
+    loss_out, loss_in1, loss_in3,
     load_sem, send_sem, recv_sem, lsend_sem, lrecv_sem, near_sem,
 ):
     rows, width = img_x.shape
@@ -59,10 +63,22 @@
     load_img.start()
     load_txt.start()
 
-    around = [right, left, sibling, at_y(1), at_y(ny - 1), at_z(1), at_z(nz - 1)]
+    near = [right, left, sibling, at_y(1), at_y(ny - 1)]
     barrier = pltpu.get_barrier_semaphore()
-    for peer in around:
-        pl.semaphore_signal(barrier, inc=1, device_id=peer, device_id_type=MESH)
+
+    def signal(semaphore, peers):
+        for peer in peers:
+            pl.semaphore_signal(semaphore, inc=1, device_id=peer, device_id_type=MESH)
+
+    def signal_if(condition, semaphore, peer):
+        @pl.when(condition)
+        def _():
+            signal(semaphore, [peer])
+
+    first_plane, last_plane = z == 0, z == nz - 1
+    signal(barrier, near)
+    signal_if(jnp.logical_not(last_plane), barrier, at_z(1))
+    signal_if(first_plane, barrier, at_z(nz - 1))
 
     def send(index, source, target, peer):
         copy = pltpu.make_async_remote_copy(
@@ -87,7 +103,7 @@
 
     load_img.wait()
     normalize(img_x, img_inv, img_all)
-    pl.semaphore_wait(barrier, len(around))
+    pl.semaphore_wait(barrier, len(near) + jnp.where(first_plane, 0, 1) + jnp.where(last_plane, 1, 0))
     right_a = send(0, img_all.at[a], img_all.at[slot(1, 0, half)], right)
     left_b = send(2, img_all.at[b], img_all.at[slot(2, half, half)], left)
     right_b = send(1, img_all.at[b], img_all.at[slot(1, half, half)], right)
@@ -97,10 +113,12 @@
     txt_part = send(7, txt_all.at[slot(0)], txt_all.at[slot(2)], partner)
     txt_sib = send(6, txt_all.at[slot(0)], txt_all.at[slot(1)], sibling)
 
-    for index, group in enumerate((around, [at_z(2), at_z(nz - 2), sibling], [at_z(4), at_z(nz - 4)])):
-        for peer in group:
-            pl.semaphore_signal(near_sem.at[index], inc=1, device_id=peer, device_id_type=MESH)
-        pl.semaphore_wait(near_sem.at[index], len(group))
+    def round_of(index, peers):
+        signal(near_sem.at[index], peers)
+
+    round_of(0, near)
+    signal_if(jnp.logical_not(first_plane), near_sem.at[0], at_z(nz - 1))
+    signal_if(last_plane, near_sem.at[0], at_z(1))
 
     right_a.wait_recv()
     pass_right = send(4, img_all.at[slot(1, 0, half)], img_all.at[slot(3, 0, half)], right)
@@ -108,21 +126,35 @@
     pass_left = send(5, img_all.at[slot(2, half, half)], img_all.at[slot(3, half, half)], left)
     txt_part.wait_recv()
     txt_diag = send(8, txt_all.at[slot(2)], txt_all.at[slot(3)], sibling)
+    pl.semaphore_wait(near_sem.at[0], len(near) + jnp.where(last_plane, 0, 1) + jnp.where(first_plane, 1, 0))
+    round_of(1, [at_x(2), at_y(2), sibling, at_z(1), at_z(nz - 1)])
 
     log_scale = jnp.full((1, 4 * rows), log_scale_ref[0], F32)
     scale = jnp.exp(log_scale)
     offset = jnp.full((1, 4 * rows), bias_ref[0], F32)
 
-    def weights(index):
+    def diagonal(shape):
+        return lax.broadcasted_iota(jnp.int32, shape, 0) == lax.broadcasted_iota(jnp.int32, shape, 1)
+
+    def logits_of(index):
         logits = scale * nt_dot(img_all[slot(index), :], txt_all[...]) + offset
         logit[slot(index), :] = logits
+
+    def loss_of(index):
+        logits = logit[slot(index), :]
+        flip = jnp.maximum(logits, 0.0)
+        if index == 0:
+            flip = jnp.where(diagonal(logits.shape), jnp.maximum(-logits, 0.0), flip)
+        terms = flip + jnp.log1p(jnp.exp(-jnp.abs(logits)))
+        return jnp.sum(terms.reshape(rows // 8, 8, 4 * rows), axis=0)
+
+    def weights(index):
+        logits = logit[slot(index), :]
         small = jnp.exp(-jnp.abs(logits))
         inv = 1.0 / (1.0 + small)
         value = jnp.where(logits >= 0, 1.0, small) * inv
         if index == 0:
-            mine = (lax.broadcasted_iota(jnp.int32, value.shape, 0)
-                    == lax.broadcasted_iota(jnp.int32, value.shape, 1))
-            value = jnp.where(mine, -jnp.where(logits >= 0, small, 1.0) * inv, value)
+            value = jnp.where(diagonal(value.shape), -jnp.where(logits >= 0, small, 1.0) * inv, value)
         weight[slot(index), :] = value.astype(BF)
 
     def img_term(index, start):
@@ -136,56 +168,22 @@
 
     txt_sib.wait_recv()
     txt_diag.wait_recv()
+    logits_of(0)
+    total = loss_of(0)
     weights(0)
     right_b.wait_recv()
     left_a.wait_recv()
-    weights(1)
-    weights(2)
-    for start, cols in chunks:
-        term = img_term(2, start)
-        hold_p[0:half, cols] = term[0:half]
-        out_right[:, cols] = term[half:].astype(BF)
-    to_right = send(11, out_right, fin_left.at[b], right)
-    for start, cols in chunks:
-        term = img_term(1, start)
-        hold_p[half:, cols] = term[half:]
-        out_left[:, cols] = term[0:half].astype(BF)
-    to_left = send(12, out_left, fin_right.at[a], left)
-    for start, cols in chunks:
-        own_p[:, cols] = img_term(0, start)
-
+    for index in (1, 2):
+        logits_of(index)
+        total = total + loss_of(index)
+        weights(index)
+    pl.semaphore_wait(near_sem.at[1], 5)
+    round_of(2, [sibling, at_z(2), at_z(nz - 2)])
     pass_right.wait_recv()
     pass_left.wait_recv()
-    weights(3)
-    for start, cols in chunks:
-        out_opp[:, cols] = img_term(3, start).astype(BF)
-    opp_right = send(9, out_opp.at[a], way_x.at[a], right)
-    opp_left = send(10, out_opp.at[b], way_x.at[b], left)
-    for start, cols in chunks:
-        out_diag[:, cols] = txt_term(3, start).astype(BF)
-    diag = send(15, out_diag, way_t, sibling)
-    for start, cols in chunks:
-        out_sib[:, cols] = txt_term(1, start).astype(BF)
-    sib = send(16, out_sib, fin_sib, sibling)
-    for start, cols in chunks:
-        hold_q[:, cols] = txt_term(2, start)
-    for start, cols in chunks:
-        own_q[:, cols] = txt_term(0, start)
-
-    total = jnp.zeros((8, 4 * rows), F32)
-    step = 64
-    for start in range(0, 4 * rows, step):
-        logits = logit[start : start + step, :]
-        flip = jnp.maximum(logits, 0.0)
-        if start < rows:
-            mine = (lax.broadcasted_iota(jnp.int32, logits.shape, 0) + start
-                    == lax.broadcasted_iota(jnp.int32, logits.shape, 1))
-            flip = jnp.where(mine, jnp.maximum(-logits, 0.0), flip)
-        terms = flip + jnp.log1p(jnp.exp(-jnp.abs(logits)))
-        total = total + jnp.sum(terms.reshape(step // 8, 8, 4 * rows), axis=0)
-    total = jnp.sum(total, axis=0, keepdims=True)
+    logits_of(3)
+    total = jnp.sum(total + loss_of(3), axis=0, keepdims=True)
     total = sum(total[:, k * rows : (k + 1) * rows] for k in range(4))
-
     lsent = []
 
     def spread(base, value, stage, inbox, peers):
@@ -207,8 +205,41 @@
             value = value + inbox[k]
         return value
 
-    plane = [at_x(step, core) for core in range(2) for step in range(nx) if step or core]
+    plane = [
+        {**at_x(dx, dc), **at_y(dy)}
+        for dy in range(ny) for dx in range(nx) for dc in range(2) if dy or dx or dc
+    ]
+    pl.semaphore_wait(near_sem.at[2], 3)
+    round_of(3, [at_z(4), at_z(nz - 4)])
     first = spread(0, total, 0, loss_in1, plane)
+    weights(3)
+    for start, cols in chunks:
+        term = img_term(2, start)
+        hold_p[0:half, cols] = term[0:half]
+        out_right[:, cols] = term[half:].astype(BF)
+    to_right = send(11, out_right, fin_left.at[b], right)
+    for start, cols in chunks:
+        term = img_term(1, start)
+        hold_p[half:, cols] = term[half:]
+        out_left[:, cols] = term[0:half].astype(BF)
+    to_left = send(12, out_left, fin_right.at[a], left)
+    for start, cols in chunks:
+        own_p[:, cols] = img_term(0, start)
+
+    for start, cols in chunks:
+        out_opp[:, cols] = img_term(3, start).astype(BF)
+    opp_right = send(9, out_opp.at[a], way_x.at[a], right)
+    opp_left = send(10, out_opp.at[b], way_x.at[b], left)
+    for start, cols in chunks:
+        out_diag[:, cols] = txt_term(3, start).astype(BF)
+    diag = send(15, out_diag, way_t, sibling)
+    for start, cols in chunks:
+        out_sib[:, cols] = txt_term(1, start).astype(BF)
+    sib = send(16, out_sib, fin_sib, sibling)
+    for start, cols in chunks:
+        hold_q[:, cols] = txt_term(2, start)
+    for start, cols in chunks:
+        own_q[:, cols] = txt_term(0, start)
 
     diag.wait_recv()
     for start, cols in chunks:
@@ -216,7 +247,8 @@
     part = send(17, out_part, fin_part, partner)
 
     total = gather(total, first, loss_in1)
-    second = spread(len(plane), total, 1, loss_in2, [at_y(step) for step in range(1, ny)])
+    pl.semaphore_wait(near_sem.at[3], 2)
+    third = spread(len(plane), total, 1, loss_in3, [at_z(step) for step in range(1, nz)])
 
     opp_right.wait_recv()
     out_comb[a] = (hold_p[a] + way_x[a].astype(F32)).astype(BF)
@@ -224,9 +256,6 @@
     opp_left.wait_recv()
     out_comb[b] = (hold_p[b] + way_x[b].astype(F32)).astype(BF)
     comb_left = send(14, out_comb.at[b], fin_right.at[b], left)
-
-    total = gather(total, second, loss_in2)
-    third = spread(len(plane) + ny - 1, total, 2, loss_in3, [at_z(step) for step in range(1, nz)])
 
     scale = jnp.exp(jnp.full((1, width), log_scale_ref[0], F32))
 
@@ -250,7 +279,7 @@
 
     total = gather(total, third, loss_in3)
     count = rows * 4 * nx * nyh * nz
-    loss_ref[0] = jnp.sum(total) * (1.0 / count)
+    loss_ref[...] = total * (1.0 / count)
 
     for copy in (
         right_a, left_b, right_b, left_a, txt_part, txt_sib, pass_right, pass_left, txt_diag, to_right, to_left,
@@ -259,11 +288,24 @@
         copy.wait_send()
 
 
+def write(loss_row, img_grad, txt_grad, loss_ref, img_out, txt_out, sems):
+    copies = [
+        pltpu.make_async_copy(img_grad, img_out, sems.at[0]),
+        pltpu.make_async_copy(txt_grad, txt_out, sems.at[1]),
+    ]
+    for copy in copies:
+        copy.start()
+    loss_ref[0] = jnp.sum(loss_row[...])
+    for copy in copies:
+        copy.wait()
+
+
 def local(image_embed, text_embed, log_scale, bias):
     rows, width = image_embed.shape
     half = rows // 2
     nx, ny, nz = lax.axis_size("x"), 2 * lax.axis_size("yh"), lax.axis_size("z")
-    peers = 2 * nx - 1 + ny - 1 + nz - 1
+    plane = 2 * nx * ny - 1
+    peers = plane + nz - 1
     smem = pl.BlockSpec(memory_space=pltpu.SMEM)
     hbm = pl.BlockSpec(memory_space=pltpu.HBM)
     vmem = pl.BlockSpec(memory_space=pltpu.VMEM)
@@ -271,15 +313,15 @@
     wide = pltpu.VMEM((rows, width), F32)
     part = pltpu.VMEM((half, width), BF)
     column = pltpu.VMEM((rows, 1), F32)
-    return pl.pallas_call(
+    loss_row, img_grad, txt_grad = pl.pallas_call(
         kernel,
         out_shape=(
-            jax.ShapeDtypeStruct((1,), F32),
+            jax.ShapeDtypeStruct((1, 128), F32),
             jax.ShapeDtypeStruct((rows, width), F32),
             jax.ShapeDtypeStruct((rows, width), F32),
         ),
         in_specs=[smem, smem, hbm, hbm],
-        out_specs=(smem, vmem, vmem),
+        out_specs=(vmem, vmem, vmem),
         scratch_shapes=[
             wide, wide, column, column,
             pltpu.VMEM((4 * rows, width), BF), pltpu.VMEM((4 * rows, width), BF),
@@ -287,18 +329,30 @@
             wide, wide, wide, wide,
             part, part, block, block, block, block, block,
             block, block, block, block, block, block,
-            pltpu.VMEM((1, 128), F32), pltpu.VMEM((3, 1, 128), F32),
-            pltpu.VMEM((2 * nx - 1, 1, 128), F32), pltpu.VMEM((ny - 1, 1, 128), F32),
+            pltpu.VMEM((2, 1, 128), F32), pltpu.VMEM((plane, 1, 128), F32),
             pltpu.VMEM((max(nz - 1, 1), 1, 128), F32),
             pltpu.SemaphoreType.DMA((2,)), pltpu.SemaphoreType.DMA((18,)), pltpu.SemaphoreType.DMA((18,)),
             pltpu.SemaphoreType.DMA((peers,)), pltpu.SemaphoreType.DMA((peers,)),
-            pltpu.SemaphoreType.REGULAR((3,)),
+            pltpu.SemaphoreType.REGULAR((4,)),
         ],
         compiler_params=pltpu.CompilerParams(
             collective_id=0, has_side_effects=True, vmem_limit_bytes=48 * 1024 * 1024
         ),
         name="siglip",
-    )(log_scale, bias, image_embed, text_embed)
+    )(log_scale, bias, in_hbm(image_embed), in_hbm(text_embed))
+    return pl.pallas_call(
+        write,
+        out_shape=(
+            jax.ShapeDtypeStruct((1,), F32),
+            jax.ShapeDtypeStruct((rows, width), F32),
+            jax.ShapeDtypeStruct((rows, width), F32),
+        ),
+        in_specs=[vmem, vmem, vmem],
+        out_specs=(smem, hbm, hbm),
+        scratch_shapes=[pltpu.SemaphoreType.DMA((2,))],
+        compiler_params=pltpu.CompilerParams(vmem_limit_bytes=2 * 1024 * 1024),
+        name="write",
+    )(loss_row, img_grad, txt_grad)
 
 
 def solution(mesh):

time: 53.1 us -> 44.4 us (0.84); the launches traced: 52.8 us -> 43.6 us
  local copies, waits for them, and re-layouts: 3.75 us -> 0 us
  Pallas kernels: 45.4 us -> 41.7 us
  between operations: 3.7 us -> 1.93 us
    unnamed x6 -> x0, local copies, waits for them, and re-layouts: 3.75 us -> none
    pallas_call x1 -> x2, Pallas kernels: 45.4 us -> 41.7 us  [the longest x1 40.1 us: local(): pl.pallas_call(kernel, out_shape=(jax.ShapeDtypeStruct((1, 128), F32), ja...]
where the time goes in v2:
time: 44.4 us; the launch traced here: 43.6 us
  Pallas kernels  41.7 us (94%)
  between operations  1.93 us (4%)
    pallas_call x1, Pallas kernels, local(): pl.pallas_call(kernel, out_shape=(jax.ShapeDtypeStruct((1, 128), F32), ja...  40.1 us
    pallas_call x1, Pallas kernels, local(): pl.pallas_call(write, out_shape=(jax.ShapeDtypeStruct((1,), F32), jax.Sha...  1.54 us

profile of v2, /device:TPU:1, one launch (start us, length us, event | category | flops | bytes accessed | tf_op | source)
XLA Modules:
  0.0 43.6 jit_solution(186008614858943038)
XLA Ops:
  1.9 40.1 %siglip.1 = (f32[1,128]{1,0:T(1,128)S(1)}, f32[128,1152]{1,0:T(8,128)S(1)}, f32[128,1152]{1,0:T(8,128)S(1)}) custom-call(f32[1]{0:T(128)S(6)} %copy.7.log_scale_ref, f32[1]{0:T(128)S(6)} %copy.8.bias_ref, f32[128,1152]{1,0:T(8,128)} %img_hbm.1, f32[128,1152]{1,0:T(8,128)} %txt_hbm.1), custom_call_target="tpu_custom_call" | custom-call | tf_op jit(solution)/shard_map/siglip/pallas_call | solution.py:316
  42.0 1.5 %write.1 = (f32[1]{0:T(128)}, f32[128,1152]{1,0:T(8,128)}, f32[128,1152]{1,0:T(8,128)}) custom-call(f32[1,128]{1,0:T(1,128)S(1)} %get-tuple-element.6.loss_row, f32[128,1152]{1,0:T(8,128)S(1)} %get-tuple-element.7.img_grad, f32[128,1152]{1,0:T(8,128)S(1)} %get-tuple-element.8.txt_grad), custom_call_target="tpu_custom_call" | custom-call | tf_op jit(solution)/shard_map/write/pallas_call | solution.py:343

commit v3 on v2

--- a/solution.py
+++ b/solution.py
@@ -1,4 +1,4 @@
-import functools
+import itertools
 
 import jax
 import jax.numpy as jnp
@@ -70,15 +70,16 @@
         for peer in peers:
             pl.semaphore_signal(semaphore, inc=1, device_id=peer, device_id_type=MESH)
 
-    def signal_if(condition, semaphore, peer):
+    def signal_if(condition, semaphore, peers):
         @pl.when(condition)
         def _():
-            signal(semaphore, [peer])
-
-    first_plane, last_plane = z == 0, z == nz - 1
+            signal(semaphore, peers)
+
+    first_plane = z == 0
+    later_plane = jnp.logical_not(first_plane)
+    others = [at_z(step) for step in range(1, nz)]
     signal(barrier, near)
-    signal_if(jnp.logical_not(last_plane), barrier, at_z(1))
-    signal_if(first_plane, barrier, at_z(nz - 1))
+    signal_if(first_plane, barrier, others)
 
     def send(index, source, target, peer):
         copy = pltpu.make_async_remote_copy(
@@ -103,7 +104,7 @@
 
     load_img.wait()
     normalize(img_x, img_inv, img_all)
-    pl.semaphore_wait(barrier, len(near) + jnp.where(first_plane, 0, 1) + jnp.where(last_plane, 1, 0))
+    pl.semaphore_wait(barrier, len(near) + jnp.where(first_plane, 0, 1))
     right_a = send(0, img_all.at[a], img_all.at[slot(1, 0, half)], right)
     left_b = send(2, img_all.at[b], img_all.at[slot(2, half, half)], left)
     right_b = send(1, img_all.at[b], img_all.at[slot(1, half, half)], right)
@@ -117,8 +118,7 @@
         signal(near_sem.at[index], peers)
 
     round_of(0, near)
-    signal_if(jnp.logical_not(first_plane), near_sem.at[0], at_z(nz - 1))
-    signal_if(last_plane, near_sem.at[0], at_z(1))
+    signal_if(later_plane, near_sem.at[3], [{"z": 0}])
 
     right_a.wait_recv()
     pass_right = send(4, img_all.at[slot(1, 0, half)], img_all.at[slot(3, 0, half)], right)
@@ -126,8 +126,8 @@
     pass_left = send(5, img_all.at[slot(2, half, half)], img_all.at[slot(3, half, half)], left)
     txt_part.wait_recv()
     txt_diag = send(8, txt_all.at[slot(2)], txt_all.at[slot(3)], sibling)
-    pl.semaphore_wait(near_sem.at[0], len(near) + jnp.where(last_plane, 0, 1) + jnp.where(first_plane, 1, 0))
-    round_of(1, [at_x(2), at_y(2), sibling, at_z(1), at_z(nz - 1)])
+    pl.semaphore_wait(near_sem.at[0], len(near))
+    round_of(1, [at_x(2), at_y(2), sibling])
 
     log_scale = jnp.full((1, 4 * rows), log_scale_ref[0], F32)
     scale = jnp.exp(log_scale)
@@ -177,41 +177,48 @@
         logits_of(index)
         total = total + loss_of(index)
         weights(index)
-    pl.semaphore_wait(near_sem.at[1], 5)
-    round_of(2, [sibling, at_z(2), at_z(nz - 2)])
+    pl.semaphore_wait(near_sem.at[1], 3)
+    round_of(2, [sibling])
     pass_right.wait_recv()
     pass_left.wait_recv()
     logits_of(3)
     total = jnp.sum(total + loss_of(3), axis=0, keepdims=True)
     total = sum(total[:, k * rows : (k + 1) * rows] for k in range(4))
-    lsent = []
-
-    def spread(base, value, stage, inbox, peers):
-        loss_out[stage] = value
-        copies = []
-        for k, peer in enumerate(peers):
-            copy = pltpu.make_async_remote_copy(
+
+    def messages(base, stage, inbox, peers):
+        return [
+            pltpu.make_async_remote_copy(
                 src_ref=loss_out.at[stage], dst_ref=inbox.at[k], send_sem=lsend_sem.at[base + k],
                 recv_sem=lrecv_sem.at[base + k], device_id=peer, device_id_type=MESH,
             )
+            for k, peer in enumerate(peers)
+        ]
+
+    def spread(value, stage, copies):
+        loss_out[stage] = value
+        for copy in reversed(copies):
             copy.start()
-            copies.append(copy)
-        lsent.extend(copies)
-        return copies
-
-    def gather(value, copies, inbox):
+
+    def gather(stage, copies, inbox):
+        value = loss_out[stage]
         for k, copy in enumerate(copies):
             copy.wait_recv()
             value = value + inbox[k]
         return value
 
+    def hops(step):
+        dy, dx, dc = step
+        return min(dy, ny - dy) + min(dx, nx - dx) + dc / 2
+
     plane = [
         {**at_x(dx, dc), **at_y(dy)}
-        for dy in range(ny) for dx in range(nx) for dc in range(2) if dy or dx or dc
+        for dy, dx, dc in sorted(itertools.product(range(ny), range(nx), range(2)), key=hops)[1:]
     ]
-    pl.semaphore_wait(near_sem.at[2], 3)
-    round_of(3, [at_z(4), at_z(nz - 4)])
-    first = spread(0, total, 0, loss_in1, plane)
+    along = sorted(range(1, nz), key=lambda step: min(step, nz - step))
+    first = messages(0, 0, loss_in1, plane)
+    third = messages(len(plane), 1, loss_in3, [at_z(step) for step in along])
+    pl.semaphore_wait(near_sem.at[2], 1)
+    spread(total, 0, first)
     weights(3)
     for start, cols in chunks:
         term = img_term(2, start)
@@ -246,9 +253,19 @@
         out_part[:, cols] = (hold_q[:, cols] + way_t[:, cols].astype(F32)).astype(BF)
     part = send(17, out_part, fin_part, partner)
 
-    total = gather(total, first, loss_in1)
-    pl.semaphore_wait(near_sem.at[3], 2)
-    third = spread(len(plane), total, 1, loss_in3, [at_z(step) for step in range(1, nz)])
+    @pl.when(first_plane)
+    def _():
+        if nz > 1:
+            pl.semaphore_wait(near_sem.at[3], nz - 1)
+            signal(near_sem.at[4], others)
+
+    total = gather(0, first, loss_in1)
+
+    @pl.when(later_plane)
+    def _():
+        pl.semaphore_wait(near_sem.at[4], 1)
+
+    spread(total, 1, third)
 
     opp_right.wait_recv()
     out_comb[a] = (hold_p[a] + way_x[a].astype(F32)).astype(BF)
@@ -277,13 +294,13 @@
     comb_left.wait_recv()
     back(own_p, fin_left, fin_right, img_x, img_inv, img_grad)
 
-    total = gather(total, third, loss_in3)
+    total = gather(1, third, loss_in3)
     count = rows * 4 * nx * nyh * nz
     loss_ref[...] = total * (1.0 / count)
 
     for copy in (
         right_a, left_b, right_b, left_a, txt_part, txt_sib, pass_right, pass_left, txt_diag, to_right, to_left,
-        opp_right, opp_left, diag, sib, part, comb_right, comb_left, *lsent,
+        opp_right, opp_left, diag, sib, part, comb_right, comb_left, *first, *third,
     ):
         copy.wait_send()
 
@@ -333,7 +350,7 @@
             pltpu.VMEM((max(nz - 1, 1), 1, 128), F32),
             pltpu.SemaphoreType.DMA((2,)), pltpu.SemaphoreType.DMA((18,)), pltpu.SemaphoreType.DMA((18,)),
             pltpu.SemaphoreType.DMA((peers,)), pltpu.SemaphoreType.DMA((peers,)),
-            pltpu.SemaphoreType.REGULAR((4,)),
+            pltpu.SemaphoreType.REGULAR((5,)),
         ],
         compiler_params=pltpu.CompilerParams(
             collective_id=0, has_side_effects=True, vmem_limit_bytes=48 * 1024 * 1024

time: 44.4 us -> 41.7 us (0.939); the launches traced: 43.6 us -> 41.6 us
  Pallas kernels: 41.7 us -> 39.6 us
    pallas_call x1, Pallas kernels: 40.1 us -> 38.1 us  [local(): pl.pallas_call(kernel, out_shape=(jax.ShapeDtypeStruct((1, 128), F32), ja...]
where the time goes in v3:
time: 41.7 us; the launch traced here: 41.6 us
  Pallas kernels  39.6 us (95%)
  between operations  1.93 us (5%)
    pallas_call x1, Pallas kernels, local(): pl.pallas_call(kernel, out_shape=(jax.ShapeDtypeStruct((1, 128), F32), ja...  38.1 us
    pallas_call x1, Pallas kernels, local(): pl.pallas_call(write, out_shape=(jax.ShapeDtypeStruct((1,), F32), jax.Sha...  1.54 us

profile of v3, /device:TPU:1, one launch (start us, length us, event | category | flops | bytes accessed | tf_op | source)
XLA Modules:
  0.0 41.6 jit_solution(8765613097977208111)
XLA Ops:
  1.9 38.1 %siglip.1 = (f32[1,128]{1,0:T(1,128)S(1)}, f32[128,1152]{1,0:T(8,128)S(1)}, f32[128,1152]{1,0:T(8,128)S(1)}) custom-call(f32[1]{0:T(128)S(6)} %copy.7.log_scale_ref, f32[1]{0:T(128)S(6)} %copy.8.bias_ref, f32[128,1152]{1,0:T(8,128)} %img_hbm.1, f32[128,1152]{1,0:T(8,128)} %txt_hbm.1), custom_call_target="tpu_custom_call" | custom-call | tf_op jit(solution)/shard_map/siglip/pallas_call | solution.py:333
  40.0 1.5 %write.1 = (f32[1]{0:T(128)}, f32[128,1152]{1,0:T(8,128)}, f32[128,1152]{1,0:T(8,128)}) custom-call(f32[1,128]{1,0:T(1,128)S(1)} %get-tuple-element.6.loss_row, f32[128,1152]{1,0:T(8,128)S(1)} %get-tuple-element.7.img_grad, f32[128,1152]{1,0:T(8,128)S(1)} %get-tuple-element.8.txt_grad), custom_call_target="tpu_custom_call" | custom-call | tf_op jit(solution)/shard_map/write/pallas_call | solution.py:360
